TPU v7x, 64 devices: a 2x2x8 block of a 4x4x8 slice. The times are simulated.
64 devices in a mesh: batch: 4 (over x, y), rows: 16 (over z, core).
Axes of the slice: x: 2, y: 2, z: 8, core: 2. Of those that a mesh axis runs over, the one named last changes fastest.
The devices are a block of a 4x4x8 slice.
Arguments:
- a_mat: float32 [524288, 640], P(('batch', 'rows')), parts along dimension 0
- rhs: float32 [524288, 64], P(('batch', 'rows')), parts along dimension 0
Outputs:
- output 1: float32 [2560, 64], P('batch'), parts along dimension 0
- output 2: float32 [2560, 640], P('batch'), parts along dimension 0
There are 4 independent parts. A program takes and returns all parts, laid end to end along the dimension named above; each array names one.
All inputs are finite; a program needn't handle non-finite values.
Results may differ from a plain program's by a relative error of at most 0.001.
Values sent between devices are 32-bit elements.
A program may use at most 768 MiB of HBM per device.

v0:
```python
import jax
import jax.numpy as jnp
from jax import lax
from jax.sharding import PartitionSpec as P

HIGHEST = lax.Precision.HIGHEST


def gram_of(left_mat, right_mat):
    return lax.dot_general(left_mat, right_mat, (((0,), (0,)), ((), ())), precision=HIGHEST, preferred_element_type=jnp.float32)


def solution(mesh):
    def group_solve(a_blk, b_blk):
        gram_one = lax.psum(gram_of(a_blk, a_blk), "rows")
        low_one = jnp.linalg.cholesky(gram_one)
        q_one = lax.linalg.triangular_solve(low_one, a_blk, left_side=False, lower=True, transpose_a=True)
        gram_two, proj_one = lax.psum((gram_of(q_one, q_one), gram_of(q_one, b_blk)), "rows")
        low_two = jnp.linalg.cholesky(gram_two)
        proj_two = lax.linalg.triangular_solve(low_two, proj_one, left_side=True, lower=True)
        low_prod = jnp.dot(low_one, low_two, precision=HIGHEST, preferred_element_type=jnp.float32)
        x_sol = lax.linalg.triangular_solve(low_prod, proj_two, left_side=True, lower=True, transpose_a=True)
        return x_sol, low_prod.T

    row_spec = P(("batch", "rows"), None)
    out_spec = P("batch", None)
    return jax.shard_map(group_solve, mesh=mesh, in_specs=(row_spec, row_spec), out_specs=(out_spec, out_spec), check_vma=False)
```

profile of v0, /device:TPU:21, one launch (start us, length us, event | category | flops | bytes accessed | tf_op | source)
XLA Modules:
  0.0 964.2 jit_solution(16831842375255172731)
XLA Ops:
  7.3 59.9 %fusion.134 = f32[640,640]{0,1:T(8,128)} fusion(f32[8192,640]{1,0:T(8,128)} %param.3), kind=kOutput, calls=%fused_computation.231 | convolution fusion | flops 40265318400 | bytes 22609920 | tf_op jit(solution)/shard_map/dot_general | solution.py:10
  67.3 112.2 %all-reduce.5.cloned.1.call-done = f32[640,640]{0,1:T(8,128)} async-done(((f32[640,640]{0,1:T(8,128)}), f32[640,640]{0,1:T(8,128)}) %all-reduce.5.cloned.1.call-update) | async-done | bytes 1638416 | tf_op jit(solution)/shard_map/psum | solution.py:15
  185.5 11.7 %cholesky.364 = f32[128,128]{1,0:T(8,128)S(1)} custom-call(f32[128,128]{1,0:T(8,128)S(1)} %cholesky.542), custom_call_target="Cholesky" | custom-call | tf_op jit(solution)/shard_map/jit(cholesky)/cholesky | solution.py:16
  197.2 9.8 %custom-call.42 = f32[1,128,128]{1,2,0:T(8,128)S(1)} custom-call(f32[1,128,128]{2,1,0:T(8,128)S(1)} %get-tuple-element.86), custom_call_target="InvertDiagBlocksLowerTriangular" | custom-call | tf_op jit(solution)/shard_map/jit(cholesky)/cholesky | solution.py:16
  211.7 11.7 %cholesky.383 = f32[128,128]{1,0:T(8,128)S(1)} custom-call(f32[128,128]{1,0:T(8,128)S(1)} %cholesky.546), custom_call_target="Cholesky" | custom-call | tf_op jit(solution)/shard_map/jit(cholesky)/cholesky | solution.py:16
  224.0 9.9 %custom-call.43 = f32[1,128,128]{1,2,0:T(8,128)S(1)} custom-call(f32[1,128,128]{2,1,0:T(8,128)S(1)} %get-tuple-element.83), custom_call_target="InvertDiagBlocksLowerTriangular" | custom-call | tf_op jit(solution)/shard_map/jit(cholesky)/cholesky | solution.py:16
  236.6 11.7 %cholesky.404 = f32[128,128]{1,0:T(8,128)S(1)} custom-call(f32[128,128]{1,0:T(8,128)S(1)} %cholesky.551), custom_call_target="Cholesky" | custom-call | tf_op jit(solution)/shard_map/jit(cholesky)/cholesky | solution.py:16
  249.6 9.8 %custom-call.44 = f32[1,128,128]{1,2,0:T(8,128)S(1)} custom-call(f32[1,128,128]{2,1,0:T(8,128)S(1)} %get-tuple-element.80), custom_call_target="InvertDiagBlocksLowerTriangular" | custom-call | tf_op jit(solution)/shard_map/jit(cholesky)/cholesky | solution.py:16
  261.9 11.9 %cholesky.423 = f32[128,128]{1,0:T(8,128)S(1)} custom-call(f32[128,128]{1,0:T(8,128)S(1)} %cholesky.556), custom_call_target="Cholesky" | custom-call | tf_op jit(solution)/shard_map/jit(cholesky)/cholesky | solution.py:16
  275.2 9.8 %custom-call.45 = f32[1,128,128]{1,2,0:T(8,128)S(1)} custom-call(f32[1,128,128]{2,1,0:T(8,128)S(1)} %get-tuple-element.77), custom_call_target="InvertDiagBlocksLowerTriangular" | custom-call | tf_op jit(solution)/shard_map/jit(cholesky)/cholesky | solution.py:16
  287.2 11.7 %cholesky.440 = f32[128,128]{1,0:T(8,128)S(1)} custom-call(f32[128,128]{1,0:T(8,128)S(1)} %convolution_subtract_fusion.9), custom_call_target="Cholesky" | custom-call | tf_op jit(solution)/shard_map/jit(cholesky)/cholesky | solution.py:16
  306.9 14.7 %while.3 = (s32[]{:T(128)}, f32[640,640]{1,0:T(8,128)}, s32[5,2]{0,1:T(2,128)S(1)}, f32[5,128,128]{2,1,0:T(8,128)S(1)}, s32[]{:T(128)}) while((s32[]{:T(128)}, f32[640,640]{1,0:T(8,128)}, s32[5,2]{0,1:T(2,128)S(1)}, f32[5,128,128]{2,1,0:T(8,128)S(1)}, s32[]{:T(128)}) %tuple.77), condition=%wide.while_cond, body=%wide.while_body.sunk | while | flops 2 | bytes 131181 | solution.py:17
  321.5 49.5 %custom-call.35 = f32[5,128,128]{1,2,0:T(8,128)S(1)} custom-call(f32[5,128,128]{2,1,0:T(8,128)S(1)} %get-tuple-element.10), custom_call_target="InvertDiagBlocksLowerTriangular" | custom-call | tf_op jit(solution)/shard_map/triangular_solve | solution.py:17
  379.0 10.3 %convolution_subtract_fusion.1 = f32[8192,128]{1,0:T(8,128)S(1)} fusion(f32[128,8192]{1,0:T(8,128)S(1)} %get-tuple-element.90, f32[8192,640]{1,0:T(8,128)} %param.3, f32[640,640]{1,0:T(8,128)} %get-tuple-element.244), kind=kOutput, calls=%fused_computation.22 | convolution fusion | flops 1611661312 | bytes 12648448 | tf_op jit(solution)/shard_map/triangular_solve | solution.py:17
  394.6 17.3 %convolution_subtract_fusion = f32[8192,128]{1,0:T(8,128)S(1)} fusion(f32[8192,128]{0,1:T(8,128)S(1)} %get-tuple-element.92, f32[8192,128]{0,1:T(8,128)S(1)} %bitcast.162, f32[8192,640]{1,0:T(8,128)} %param.3, f32[640,640]{1,0:T(8,128)} %get-tuple-element.244), kind=kOutput, calls=%fused_computation.21 | convolution fusion | flops 3224371200 | bytes 16908288 | tf_op jit(solution)/shard_map/triangular_solve | solution.py:17
  417.3 25.7 %fusion.14 = f32[8192,128]{1,0:T(8,128)} fusion(f32[8192,128]{0,1:T(8,128)S(1)} %get-tuple-element.94, f32[8192,128]{0,1:T(8,128)S(1)} %get-tuple-element.92, f32[8192,128]{0,1:T(8,128)S(1)} %bitcast.163, f32[8192,640]{1,0:T(8,128)} %param.3, f32[640,640]{1,0:T(8,128)} %get-tuple-element.244), kind=kOutput, calls=%fused_computation.23 | convolution fusion | flops 4839178240 | bytes 21168128 | tf_op jit(solution)/shard_map/triangular_solve | solution.py:17
  452.3 32.5 %fusion.17 = f32[8192,128]{1,0:T(8,128)} fusion(f32[8192,128]{0,1:T(8,128)} %get-tuple-element.96, f32[8192,128]{0,1:T(8,128)} %copy-done.3, f32[8192,128]{0,1:T(8,128)} %copy-done.2, f32[8192,128]{0,1:T(8,128)} %bitcast.164, f32[8192,640]{1,0:T(8,128)} %param.3, f32[640,640]{1,0:T(8,128)} %get-tuple-element.244), kind=kOutput, calls=%fused_computation.24 | convolution fusion | flops 6456082432 | bytes 25427968 | tf_op jit(solution)/shard_map/triangular_solve | solution.py:17
  492.8 54.7 %fusion.135 = f32[640,640]{0,1:T(8,128)} fusion(f32[8192,640]{0,1:T(8,128)} %convolution_dynamic-update-slice_fusion), kind=kOutput, calls=%fused_computation.232 | convolution fusion | flops 40265318400 | bytes 22609920 | tf_op jit(solution)/shard_map/dot_general | solution.py:10
  547.5 23.8 %fusion.136 = f32[640,64]{0,1:T(8,128)} fusion(f32[8192,640]{0,1:T(8,128)} %convolution_dynamic-update-slice_fusion, f32[8192,64]{0,1:T(8,128)S(1)} %copy-done), kind=kOutput, calls=%fused_computation.233 | convolution fusion | flops 4026531840 | bytes 23232512 | tf_op jit(solution)/shard_map/dot_general | solution.py:10
  571.3 108.7 %all-reduce.7.cloned.1.call-done = (f32[640,640]{0,1:T(8,128)}, f32[640,64]{0,1:T(8,128)}) async-done(((f32[640,640]{0,1:T(8,128)}, f32[640,64]{0,1:T(8,128)}), (f32[640,640]{0,1:T(8,128)}, f32[640,64]{0,1:T(8,128)})) %all-reduce.7.cloned.1.call-update) | async-done | bytes 1802256 | tf_op jit(solution)/shard_map/psum | solution.py:18
  686.4 11.7 %cholesky.455 = f32[128,128]{1,0:T(8,128)S(1)} custom-call(f32[128,128]{1,0:T(8,128)S(1)} %cholesky.560), custom_call_target="Cholesky" | custom-call | tf_op jit(solution)/shard_map/jit(cholesky)/cholesky | solution.py:19
  699.5 9.8 %custom-call.46 = f32[1,128,128]{1,2,0:T(8,128)S(1)} custom-call(f32[1,128,128]{2,1,0:T(8,128)S(1)} %get-tuple-element.73), custom_call_target="InvertDiagBlocksLowerTriangular" | custom-call | tf_op jit(solution)/shard_map/jit(cholesky)/cholesky | solution.py:19
  712.7 11.7 %cholesky.474 = f32[128,128]{1,0:T(8,128)S(1)} custom-call(f32[128,128]{1,0:T(8,128)S(1)} %cholesky.564), custom_call_target="Cholesky" | custom-call | tf_op jit(solution)/shard_map/jit(cholesky)/cholesky | solution.py:19
  726.3 10.0 %custom-call.47 = f32[1,128,128]{1,2,0:T(8,128)S(1)} custom-call(f32[1,128,128]{2,1,0:T(8,128)S(1)} %get-tuple-element.70), custom_call_target="InvertDiagBlocksLowerTriangular" | custom-call | tf_op jit(solution)/shard_map/jit(cholesky)/cholesky | solution.py:19
  738.9 11.7 %cholesky.495 = f32[128,128]{1,0:T(8,128)S(1)} custom-call(f32[128,128]{1,0:T(8,128)S(1)} %cholesky.569), custom_call_target="Cholesky" | custom-call | tf_op jit(solution)/shard_map/jit(cholesky)/cholesky | solution.py:19
  751.9 9.8 %custom-call.48 = f32[1,128,128]{1,2,0:T(8,128)S(1)} custom-call(f32[1,128,128]{2,1,0:T(8,128)S(1)} %get-tuple-element.67), custom_call_target="InvertDiagBlocksLowerTriangular" | custom-call | tf_op jit(solution)/shard_map/jit(cholesky)/cholesky | solution.py:19
  764.3 11.9 %cholesky.514 = f32[128,128]{1,0:T(8,128)S(1)} custom-call(f32[128,128]{1,0:T(8,128)S(1)} %cholesky.574), custom_call_target="Cholesky" | custom-call | tf_op jit(solution)/shard_map/jit(cholesky)/cholesky | solution.py:19
  789.5 11.7 %cholesky.531 = f32[128,128]{1,0:T(8,128)S(1)} custom-call(f32[128,128]{1,0:T(8,128)S(1)} %convolution_subtract_fusion.8), custom_call_target="Cholesky" | custom-call | tf_op jit(solution)/shard_map/jit(cholesky)/cholesky | solution.py:19
  815.5 14.1 %while.4 = (s32[]{:T(128)}, f32[640,640]{1,0:T(8,128)}, s32[5,2]{0,1:T(2,128)S(1)}, f32[5,128,128]{2,1,0:T(8,128)S(1)}, s32[]{:T(128)}) while((s32[]{:T(128)}, f32[640,640]{1,0:T(8,128)}, s32[5,2]{0,1:T(2,128)S(1)}, f32[5,128,128]{2,1,0:T(8,128)S(1)}, s32[]{:T(128)}) %tuple.91), condition=%wide.while_cond.1, body=%wide.while_body.1.sunk | while | flops 2 | bytes 131181 | solution.py:22
  829.6 49.4 %custom-call.36 = f32[5,128,128]{1,2,0:T(8,128)S(1)} custom-call(f32[5,128,128]{2,1,0:T(8,128)S(1)} %get-tuple-element.18), custom_call_target="InvertDiagBlocksLowerTriangular" | custom-call | tf_op jit(solution)/shard_map/triangular_solve | solution.py:22
  879.0 14.1 %while.5 = (s32[]{:T(128)}, f32[640,640]{1,0:T(8,128)}, s32[5,2]{0,1:T(2,128)S(1)}, f32[5,128,128]{2,1,0:T(8,128)S(1)}, s32[]{:T(128)}) while((s32[]{:T(128)}, f32[640,640]{1,0:T(8,128)}, s32[5,2]{0,1:T(2,128)S(1)}, f32[5,128,128]{2,1,0:T(8,128)S(1)}, s32[]{:T(128)}) %tuple.92), condition=%wide.while_cond.2, body=%wide.while_body.2.sunk | while | flops 2 | bytes 131181 | solution.py:20
  893.0 49.1 %custom-call.37 = f32[5,128,128]{1,2,0:T(8,128)S(1)} custom-call(f32[5,128,128]{2,1,0:T(8,128)S(1)} %get-tuple-element.26), custom_call_target="InvertDiagBlocksLowerTriangular" | custom-call | tf_op jit(solution)/shard_map/triangular_solve | solution.py:20
  (153 shorter events, 163.3 us)
Async XLA Ops:
  7.2 540.3 %copy-start = (f32[8192,64]{0,1:T(8,128)S(1)}, f32[8192,64]{0,1:T(8,128)}, u32[]{:S(2)}) copy-start(f32[8192,64]{0,1:T(8,128)} %param.4) | copy-start | bytes 6291460
  7.2 172.3 %all-reduce.5.cloned.1.call-start = ((), (), s32[]{:S(2)}) async-start(), calls=%async_computation | async-start | bytes 3276800 | tf_op jit(solution)/shard_map/psum | solution.py:15
  67.2 612.8 %all-reduce.7.cloned.1.call-start = ((), (), s32[]{:S(2)}) async-start(), calls=%async_computation.1 | async-start | bytes 3604480 | tf_op jit(solution)/shard_map/psum | solution.py:18
  184.3 1.2 copy-start.6
  379.0 38.3 %copy-start.1 = (f32[128,8192]{1,0:T(8,128)}, f32[128,8192]{1,0:T(8,128)S(1)}, u32[]{:S(2)}) copy-start(f32[128,8192]{1,0:T(8,128)S(1)} %get-tuple-element.90) | copy-start | bytes 12582916
  394.6 22.7 %copy-start.2 = (f32[8192,128]{0,1:T(8,128)}, f32[8192,128]{0,1:T(8,128)S(1)}, u32[]{:S(2)}) copy-start(f32[8192,128]{0,1:T(8,128)S(1)} %get-tuple-element.92) | copy-start | bytes 12582916
  417.3 25.7 %copy-start.3 = (f32[8192,128]{0,1:T(8,128)}, f32[8192,128]{0,1:T(8,128)S(1)}, u32[]{:S(2)}) copy-start(f32[8192,128]{0,1:T(8,128)S(1)} %get-tuple-element.94) | copy-start | bytes 12582916
  685.2 1.2 copy-start.5
  805.7 8.4 copy-start.4
  815.5 126.7 %copy-start.7 = (f32[640,64]{0,1:T(8,128)S(1)}, f32[640,64]{0,1:T(8,128)}, u32[]{:S(2)}) copy-start(f32[640,64]{0,1:T(8,128)} %get-tuple-element.54) | copy-start | bytes 491524
  954.1 2.8 copy-start.8
Sparse Core Ops, SparseCore 0:
  67.3 112.0 all-reduce.4
  571.4 108.5 all-reduce.6
where the time goes:
time: 975 us; the launch traced here: 964 us
  other arithmetic  364 us (37%)
  matrix products  302 us (31%)
  waiting for transfers between devices  221 us (23%)
  local copies, waits for them, and re-layouts  56.2 us (6%)
  between operations  21.3 us (2%)
    dot_general x3, matrix products, gram_of(): lax.dot_general(left_mat, right_mat, (((0,), (0,)), ((), ())), precision=...  138 us
    another operation x9, matrix products, group_solve(): lax.linalg.triangular_solve(low_one, a_blk, left_side=False, lower=True,...  122 us
    psum x1, waiting for transfers between devices, group_solve(): gram_one = lax.psum(gram_of(a_blk, a_blk), 'rows')  112 us
    psum x1, waiting for transfers between devices, group_solve(): lax.psum((gram_of(q_one, q_one), gram_of(q_one, b_blk)), 'rows')  109 us
    another operation x19, other arithmetic, group_solve(): low_two = jnp.linalg.cholesky(gram_two)  104 us
    another operation x18, other arithmetic, group_solve(): low_one = jnp.linalg.cholesky(gram_one)  103 us
    another operation x3, other arithmetic, group_solve(): lax.linalg.triangular_solve(low_one, a_blk, left_side=False, lower=True,...  52.3 us
    another operation x2, other arithmetic, group_solve(): lax.linalg.triangular_solve(low_two, proj_one, left_side=True, lower=True)  50.4 us
  transfers between devices with their start and end apart: 2, of which 2 were waited for; matrix products, arithmetic and copies ran while one was open for 0% of the time, Pallas kernels for 0%

commit v1 on v0

v1 whole, which is shorter than its diff:
```python
import functools
import jax
import jax.numpy as jnp
from jax import lax
from jax.experimental import pallas as pl
from jax.experimental.pallas import tpu as pltpu
from jax.sharding import PartitionSpec as P

HIGHEST = lax.Precision.HIGHEST
MESH = pl.DeviceIdType.MESH
LEAF = 8
BLK = 128
WIDE = 256
ROW_TILE = 512
VMEM_BYTES = 64000 * 1024


def dot_f32(lhs, rhs, lhs_dim, rhs_dim):
    return lax.dot_general(lhs, rhs, (((lhs_dim,), (rhs_dim,)), ((), ())), precision=HIGHEST, preferred_element_type=jnp.float32)


def block_pairs(n):
    n_blk = n // BLK
    return [(i, j) for i in range(n_blk) for j in range(i, n_blk)]


def packed_rows(n, n_rhs, members):
    rows = len(block_pairs(n)) * BLK + (n // 2 if n_rhs else 0)
    unit = 8 * members
    return -(-rows // unit) * unit


def pack_upper(acc, out_ref, n):
    for idx, (i, j) in enumerate(block_pairs(n)):
        out_ref[idx * BLK:(idx + 1) * BLK, :] = acc[i * BLK:(i + 1) * BLK, j * BLK:(j + 1) * BLK]


def gram_kernel(a_ref, out_ref, acc):
    n = a_ref.shape[1]

    @pl.when(pl.program_id(0) == 0)
    def _():
        acc[...] = jnp.zeros_like(acc)

    for lo in range(0, n, WIDE):
        hi = min(lo + WIDE, n)
        acc[:hi, lo:hi] += dot_f32(a_ref[:, :hi], a_ref[:, lo:hi], 0, 0)

    @pl.when(pl.program_id(0) == pl.num_programs(0) - 1)
    def _():
        pack_upper(acc, out_ref, n)


def local_gram(a_blk, rows):
    m, n = a_blk.shape
    return pl.pallas_call(
        gram_kernel,
        grid=(m // ROW_TILE,),
        out_shape=jax.ShapeDtypeStruct((rows, BLK), jnp.float32),
        in_specs=[pl.BlockSpec((ROW_TILE, n), lambda t: (t, 0))],
        out_specs=pl.BlockSpec((rows, BLK), lambda t: (0, 0)),
        scratch_shapes=[pltpu.VMEM((n, n), jnp.float32)],
        compiler_params=pltpu.CompilerParams(vmem_limit_bytes=VMEM_BYTES),
        cost_estimate=pl.CostEstimate(flops=m * n * n * 6, bytes_accessed=4 * m * n, transcendentals=0),
        name="gram_one",
    )(a_blk)


def basis_kernel(a_ref, b_ref, inv_ref, out_ref, acc, proj, q_ref):
    n, n_rhs = a_ref.shape[1], b_ref.shape[1]

    @pl.when(pl.program_id(0) == 0)
    def _():
        acc[...] = jnp.zeros_like(acc)
        proj[...] = jnp.zeros_like(proj)

    for lo in range(0, n, WIDE):
        hi = min(lo + WIDE, n)
        q_ref[:, lo:hi] = dot_f32(a_ref[:, :hi], inv_ref[:hi, lo:hi], 1, 0)
    for lo in range(0, n, WIDE):
        hi = min(lo + WIDE, n)
        if hi < n:
            acc[:hi, lo:hi] += dot_f32(q_ref[:, :hi], q_ref[:, lo:hi], 0, 0)
        else:
            both = dot_f32(q_ref[...], jnp.concatenate([q_ref[:, lo:hi], b_ref[...]], axis=1), 0, 0)
            acc[:, lo:hi] += both[:, :hi - lo]
            proj[...] += both[:, hi - lo:]

    @pl.when(pl.program_id(0) == pl.num_programs(0) - 1)
    def _():
        pack_upper(acc, out_ref, n)
        base = len(block_pairs(n)) * BLK
        half = n // 2
        out_ref[base:base + half, :] = jnp.concatenate([proj[:half, :], proj[half:, :]], axis=1)
        if base + half < out_ref.shape[0]:
            out_ref[base + half:, :] = jnp.zeros((out_ref.shape[0] - base - half, BLK), jnp.float32)


def local_basis(a_blk, b_blk, r_inv, rows):
    m, n = a_blk.shape
    n_rhs = b_blk.shape[1]
    return pl.pallas_call(
        basis_kernel,
        grid=(m // ROW_TILE,),
        out_shape=jax.ShapeDtypeStruct((rows, BLK), jnp.float32),
        in_specs=[
            pl.BlockSpec((ROW_TILE, n), lambda t: (t, 0)),
            pl.BlockSpec((ROW_TILE, n_rhs), lambda t: (t, 0)),
            pl.BlockSpec((n, n), lambda t: (0, 0)),
        ],
        out_specs=pl.BlockSpec((rows, BLK), lambda t: (0, 0)),
        scratch_shapes=[pltpu.VMEM((n, n), jnp.float32), pltpu.VMEM((n, n_rhs), jnp.float32), pltpu.VMEM((ROW_TILE, n), jnp.float32)],
        compiler_params=pltpu.CompilerParams(vmem_limit_bytes=VMEM_BYTES),
        cost_estimate=pl.CostEstimate(flops=m * n * n * 12, bytes_accessed=4 * m * (n + n_rhs), transcendentals=0),
        name="basis_gram_two",
    )(a_blk, b_blk, r_inv)


def sum_kernel(members, part, out, pair_buf, acc, slots, pair_send, pair_recv, send_sems, recv_sems, back_send, back_recv, fwd_send, fwd_recv):
    chips = members // 2
    me = lax.axis_index("rows")
    core, chip = lax.rem(me, 2), lax.div(me, 2)
    half = part.shape[0] // 2
    chunk = half // chips
    pair = {"rows": chip * 2 + 1 - core}

    def peer(d):
        return lax.rem(chip + d, chips)

    def rows_at(start, size):
        return pl.ds(pl.multiple_of(start, 8), size)

    barrier = pltpu.get_barrier_semaphore()
    pl.semaphore_signal(barrier, inc=1, device_id=pair, device_id_type=MESH)
    for d in range(1, chips):
        pl.semaphore_signal(barrier, inc=1, device_id={"rows": peer(d) * 2 + core}, device_id_type=MESH)
    pl.semaphore_wait(barrier, chips)

    swap = pltpu.make_async_remote_copy(
        src_ref=part.at[rows_at((1 - core) * half, half)], dst_ref=pair_buf, send_sem=pair_send, recv_sem=pair_recv,
        device_id=pair, device_id_type=MESH)
    swap.start()
    swap.wait()
    mine = core * half
    acc[...] = part[rows_at(mine, half)] + pair_buf[...]

    out_copies = []
    for d in range(1, chips):
        copy = pltpu.make_async_remote_copy(
            src_ref=acc.at[rows_at(peer(d) * chunk, chunk)], dst_ref=slots.at[d - 1], send_sem=send_sems.at[d - 1], recv_sem=recv_sems.at[d - 1],
            device_id={"rows": peer(d) * 2 + core}, device_id_type=MESH)
        copy.start()
        out_copies.append(copy)
    for copy in out_copies:
        copy.wait()
    total = acc[rows_at(chip * chunk, chunk)]
    for d in range(1, chips):
        total = total + slots[d - 1]
    own = rows_at(mine + chip * chunk, chunk)
    out[own] = total

    back_copies = []
    for d in range(1, chips):
        copy = pltpu.make_async_remote_copy(
            src_ref=out.at[own], dst_ref=out.at[own], send_sem=back_send.at[d - 1], recv_sem=back_recv.at[d - 1],
            device_id={"rows": peer(d) * 2 + core}, device_id_type=MESH)
        copy.start()
        back_copies.append(copy)
    forwards = []
    for d in range(chips):
        if d:
            back_copies[d - 1].wait_recv()
        src = rows_at(mine + peer(chips - d) * chunk, chunk)
        copy = pltpu.make_async_remote_copy(
            src_ref=out.at[src], dst_ref=out.at[src], send_sem=fwd_send.at[d], recv_sem=fwd_recv.at[d],
            device_id=pair, device_id_type=MESH)
        copy.start()
        forwards.append(copy)
    for copy in back_copies:
        copy.wait_send()
    for copy in forwards:
        copy.wait()


def sum_over_rows(part, members, collective_id):
    rows = part.shape[0]
    chips = members // 2
    half = rows // 2
    chunk = half // chips
    sems = pltpu.SemaphoreType.DMA
    return pl.pallas_call(
        functools.partial(sum_kernel, members),
        out_shape=jax.ShapeDtypeStruct(part.shape, jnp.float32),
        in_specs=[pl.BlockSpec(memory_space=pltpu.VMEM)],
        out_specs=pl.BlockSpec(memory_space=pltpu.VMEM),
        scratch_shapes=[
            pltpu.VMEM((half, BLK), jnp.float32), pltpu.VMEM((half, BLK), jnp.float32), pltpu.VMEM((chips - 1, chunk, BLK), jnp.float32),
            sems, sems, sems((chips - 1,)), sems((chips - 1,)), sems((chips - 1,)), sems((chips - 1,)), sems((chips,)), sems((chips,)),
        ],
        compiler_params=pltpu.CompilerParams(collective_id=collective_id, has_side_effects=True),
        name="sum_over_rows",
    )(part)


def row_of(arr, idx):
    return jnp.broadcast_to(arr[idx:idx + 1, :], (LEAF, arr.shape[1]))


def factor_block(sym):
    n_leaf = BLK // LEAF
    ahead = 2
    row_id = lax.broadcasted_iota(jnp.int32, (BLK, BLK), 0)
    col_id = lax.broadcasted_iota(jnp.int32, (BLK, BLK), 1)
    eye = (row_id == col_id).astype(jnp.float32)
    sub_id = lax.broadcasted_iota(jnp.int32, (LEAF, BLK), 0)
    s_rows = [sym[LEAF * t:LEAF * (t + 1), :] for t in range(n_leaf)]
    i_rows = [eye[LEAF * t:LEAF * (t + 1), :] for t in range(n_leaf)]
    for t in range(n_leaf):
        span = list(range(t, min(t + ahead + 1, n_leaf)))
        ecol = [[jnp.broadcast_to(s_rows[u][:, LEAF * t + i:LEAF * t + i + 1], (LEAF, BLK)) for u in span] for i in range(LEAF)]
        w_s, w_i = s_rows[t], i_rows[t]
        for i in range(LEAF):
            inv = lax.rsqrt(row_of(ecol[i][0], i))
            lcol = [e * inv for e in ecol[i]]
            bc_s = row_of(s_rows[t], i) * inv
            bc_i = row_of(i_rows[t], i) * inv
            w_s = jnp.where(sub_id == i, bc_s, w_s)
            w_i = jnp.where(sub_id == i, bc_i, w_i)
            for v, u in enumerate(span):
                if v == 0 and i == LEAF - 1:
                    continue
                s_rows[u] = s_rows[u] - lcol[v] * bc_s
                i_next = i_rows[u] - lcol[v] * bc_i
                i_rows[u] = i_next if v else jnp.where(sub_id > i, i_next, i_rows[u])
            for j in range(i + 1, LEAF):
                piv = row_of(lcol[0], j)
                ecol[j] = [e - c * piv for e, c in zip(ecol[j], lcol)]
        s_rows[t], i_rows[t] = w_s, w_i
        rest = t + ahead + 1
        if rest < n_leaf:
            upd = dot_f32(w_s, jnp.concatenate([w_s, w_i], axis=1), 0, 0)
            for u in range(rest, n_leaf):
                s_rows[u] = s_rows[u] - upd[LEAF * u:LEAF * (u + 1), :BLK]
                i_rows[u] = i_rows[u] - upd[LEAF * u:LEAF * (u + 1), BLK:]
    r_blk = jnp.where(row_id <= col_id, jnp.concatenate(s_rows, axis=0), 0.0)
    linv = jnp.where(row_id >= col_id, jnp.concatenate(i_rows, axis=0), 0.0)
    return r_blk, linv


def factor_all(work, r_out, n):
    n_blk = n // BLK

    def step(k, carry):
        base = pl.multiple_of(k * BLK, BLK)
        r_blk, linv = factor_block(work[pl.ds(base, BLK), pl.ds(base, BLK)])
        for kk in range(n_blk):
            @pl.when(k == kk)
            def _():
                lo, hi = BLK * kk, BLK * (kk + 1)
                if lo:
                    work[lo:hi, :lo] = dot_f32(linv, work[lo:hi, :lo], 1, 0)
                    r_out[lo:hi, :lo] = jnp.zeros((BLK, lo), jnp.float32)
                work[lo:hi, lo:hi] = linv
                r_out[lo:hi, lo:hi] = r_blk
                if hi < n:
                    r_row = dot_f32(linv, work[lo:hi, hi:], 1, 0)
                    r_out[lo:hi, hi:] = r_row
                    work[lo:hi, hi:] = jnp.zeros((BLK, n - hi), jnp.float32)
                    for ii in range(kk + 1, n_blk):
                        a, b = BLK * ii, BLK * (ii + 1)
                        fac = r_row[:, a - hi:b - hi]
                        work[a:b, a:] = work[a:b, a:] - dot_f32(fac, r_row[:, a - hi:], 0, 0)
                        if lo:
                            work[a:b, :lo] = work[a:b, :lo] - dot_f32(fac, work[lo:hi, :lo], 0, 0)
                        work[a:b, lo:hi] = -dot_f32(fac, linv, 0, 0)
        return carry

    lax.fori_loop(0, n_blk, step, 0)


def unpack_upper(packed, work, n):
    for idx, (i, j) in enumerate(block_pairs(n)):
        work[i * BLK:(i + 1) * BLK, j * BLK:(j + 1) * BLK] = packed[idx * BLK:(idx + 1) * BLK, :]
        if i < j:
            work[j * BLK:(j + 1) * BLK, i * BLK:(i + 1) * BLK] = jnp.zeros((BLK, BLK), jnp.float32)


def factor_kernel(packed, r_out, inv_out, work):
    n = work.shape[0]
    unpack_upper(packed, work, n)
    factor_all(work, r_out, n)
    for c in range(0, n, BLK):
        inv_out[:, c:c + BLK] = work[c:c + BLK, :].T


def factor_one(packed, n):
    return pl.pallas_call(
        factor_kernel,
        out_shape=[jax.ShapeDtypeStruct((n, n), jnp.float32)] * 2,
        in_specs=[pl.BlockSpec(memory_space=pltpu.VMEM)],
        out_specs=[pl.BlockSpec(memory_space=pltpu.VMEM)] * 2,
        scratch_shapes=[pltpu.VMEM((n, n), jnp.float32)],
        name="factor_one",
    )(packed)


def finish_kernel(packed, r_one, inv_one, x_out, r_out, work, r_two):
    n, n_rhs = x_out.shape
    unpack_upper(packed, work, n)
    factor_all(work, r_two, n)
    base = len(block_pairs(n)) * BLK
    half = n // 2
    flat = packed[base:base + half, :]
    proj = jnp.concatenate([flat[:, :n_rhs], flat[:, n_rhs:]], axis=0)
    proj_two = dot_f32(work[...], proj, 1, 0)
    back = dot_f32(work[...], proj_two, 0, 0)
    x_out[...] = dot_f32(inv_one[...], back, 1, 0)
    for lo in range(0, n, BLK):
        hi = lo + BLK
        if lo:
            r_out[lo:hi, :lo] = jnp.zeros((BLK, lo), jnp.float32)
        r_out[lo:hi, lo:] = dot_f32(r_two[lo:hi, lo:], r_one[lo:, lo:], 1, 0)


def finish(packed, r_one, inv_one, n_rhs):
    n = r_one.shape[0]
    return pl.pallas_call(
        finish_kernel,
        out_shape=[jax.ShapeDtypeStruct((n, n_rhs), jnp.float32), jax.ShapeDtypeStruct((n, n), jnp.float32)],
        in_specs=[pl.BlockSpec(memory_space=pltpu.VMEM)] * 3,
        out_specs=[pl.BlockSpec(memory_space=pltpu.VMEM)] * 2,
        scratch_shapes=[pltpu.VMEM((n, n), jnp.float32)] * 2,
        name="finish",
    )(packed, r_one, inv_one)


def solution(mesh):
    members = mesh.shape["rows"]

    def group_solve(a_blk, b_blk):
        n, n_rhs = a_blk.shape[1], b_blk.shape[1]
        gram_one = sum_over_rows(local_gram(a_blk, packed_rows(n, 0, members)), members, 1)
        r_one, inv_one = factor_one(gram_one, n)
        gram_two = sum_over_rows(local_basis(a_blk, b_blk, inv_one, packed_rows(n, n_rhs, members)), members, 2)
        return finish(gram_two, r_one, inv_one, n_rhs)

    row_spec = P(("batch", "rows"), None)
    out_spec = P("batch", None)
    return jax.shard_map(group_solve, mesh=mesh, in_specs=(row_spec, row_spec), out_specs=(out_spec, out_spec), check_vma=False)
```

time: 975 us -> 287 us (0.29); the launches traced: 964 us -> 286 us
  other arithmetic: 364 us -> 0 us
  matrix products: 302 us -> 0 us
  Pallas kernels: 0 us -> 281 us
  waiting for transfers between devices: 221 us -> 0 us
  local copies, waits for them, and re-layouts: 56.2 us -> 4.49 us
  between operations: 21.3 us -> 0.65 us
    another operation x43 -> x0, other arithmetic: 360 us -> none  [the longest x19 104 us: group_solve(): low_two = jnp.linalg.cholesky(gram_two)]
    pallas_call x0 -> x6, Pallas kernels: none -> 281 us  [the longest x2 84 us: sum_over_rows(): pl.pallas_call(functools.partial(sum_kernel, members), out_shape=jax.Shap...]
    psum x2 -> x0, waiting for transfers between devices: 221 us -> none  [the longest x1 112 us: group_solve(): gram_one = lax.psum(gram_of(a_blk, a_blk), 'rows')]
    another operation x43 -> x0, matrix products: 155 us -> none  [the longest x9 122 us: group_solve(): lax.linalg.triangular_solve(low_one, a_blk, left_side=False, lower=True,...]
    dot_general x4 -> x0, matrix products: 147 us -> none  [the longest x3 138 us: gram_of(): lax.dot_general(left_mat, right_mat, (((0,), (0,)), ((), ())), precision=...]
    another operation x57 -> x0, local copies, waits for them, and re-layouts: 45.1 us -> none
  transfers between devices with their start and end apart: 2 -> 0, of which waited for: 2 -> 0; matrix products, arithmetic and copies ran while one was open for 0% -> 0% of each run, Pallas kernels for 0% -> 0%
where the time goes in v1:
time: 287 us; the launch traced here: 286 us
  Pallas kernels  281 us (98%)
  local copies, waits for them, and re-layouts  4.49 us (2%)
    pallas_call x2, Pallas kernels, sum_over_rows(): pl.pallas_call(functools.partial(sum_kernel, members), out_shape=jax.Shap...  84 us
    pallas_call x1, Pallas kernels, local_basis(): pl.pallas_call(basis_kernel, grid=(m // ROW_TILE,), out_shape=jax.ShapeDt...  82.8 us
    pallas_call x1, Pallas kernels, local_gram(): pl.pallas_call(gram_kernel, grid=(m // ROW_TILE,), out_shape=jax.ShapeDty...  44.5 us
    pallas_call x1, Pallas kernels, finish(): pl.pallas_call(finish_kernel, out_shape=[jax.ShapeDtypeStruct((n, n_rhs),...  39.3 us
    pallas_call x1, Pallas kernels, factor_one(): pl.pallas_call(factor_kernel, out_shape=[jax.ShapeDtypeStruct((n, n), jnp...  30.6 us

profile of v1, /device:TPU:21, one launch (start us, length us, event | category | flops | bytes accessed | tf_op | source)
XLA Modules:
  0.0 286.4 jit_solution(14841703522418541096)
XLA Ops:
  0.6 44.5 %gram_one.1.part = f32[1920,128]{1,0:T(8,128)} custom-call(f32[8192,640]{1,0:T(8,128)} %a_ref.3), custom_call_target="tpu_custom_call" | custom-call | flops 20132659200 | bytes 20971520 | tf_op jit(solution)/shard_map/gram_one/pallas_call | solution.py:56
  45.1 0.0 copy-start
  45.1 44.1 %sum_over_rows.2.packed = f32[1920,128]{1,0:T(8,128)} custom-call(f32[1920,128]{1,0:T(8,128)} %gram_one.1.part), custom_call_target="tpu_custom_call" | custom-call | tf_op jit(solution)/shard_map/sum_over_rows/pallas_call | solution.py:191
  89.2 30.6 %factor_one.1 = (f32[640,640]{1,0:T(8,128)}, f32[640,640]{1,0:T(8,128)}) custom-call(f32[1920,128]{1,0:T(8,128)} %sum_over_rows.2.packed), custom_call_target="tpu_custom_call" | custom-call | tf_op jit(solution)/shard_map/factor_one/pallas_call | solution.py:297
  119.8 0.0 copy-done
  119.8 2.7 copy.4.b_ref
  122.5 82.8 %basis_gram_two.1.part = f32[2304,128]{1,0:T(8,128)} custom-call(f32[8192,640]{1,0:T(8,128)} %a_ref.3, f32[8192,64]{1,0:T(8,128)} %copy.4.b_ref, f32[640,640]{1,0:T(8,128)} %get-tuple-element.4.inv_ref.inv_one), custom_call_target="tpu_custom_call" | custom-call | flops 40265318400 | bytes 23068672 | tf_op jit(solution)/shard_map/basis_gram_two/pallas_call | solution.py:102
  205.3 39.9 %sum_over_rows.3.packed = f32[2304,128]{1,0:T(8,128)} custom-call(f32[2304,128]{1,0:T(8,128)} %basis_gram_two.1.part), custom_call_target="tpu_custom_call" | custom-call | tf_op jit(solution)/shard_map/sum_over_rows/pallas_call | solution.py:191
  245.2 39.3 %finish.1 = (f32[640,64]{1,0:T(8,128)}, f32[640,640]{1,0:T(8,128)}) custom-call(f32[2304,128]{1,0:T(8,128)} %sum_over_rows.3.packed, f32[640,640]{1,0:T(8,128)} %get-tuple-element.5.r_one, f32[640,640]{1,0:T(8,128)} %get-tuple-element.4.inv_ref.inv_one), custom_call_target="tpu_custom_call" | custom-call | tf_op jit(solution)/shard_map/finish/pallas_call | solution.py:327
  284.6 1.8 copy.5
Async XLA Ops:
  45.1 74.7 %copy-start = (f32[8192,64]{0,1:T(8,128)S(1)}, f32[8192,64]{0,1:T(8,128)}, u32[]{:S(2)}) copy-start(f32[8192,64]{0,1:T(8,128)} %param.3) | copy-start | bytes 6291460

commit v2 on v0

v2 whole, which is shorter than its diff:
```python
import functools
import jax
import jax.numpy as jnp
from jax import lax
from jax.experimental import pallas as pl
from jax.experimental.pallas import tpu as pltpu
from jax.sharding import PartitionSpec as P

HIGHEST = lax.Precision.HIGHEST
MESH = pl.DeviceIdType.MESH
LEAF = 8
BLK = 128
ROW_TILE = 512
VMEM_BYTES = 64000 * 1024


def dot_f32(lhs, rhs, lhs_dim, rhs_dim):
    return lax.dot_general(lhs, rhs, (((lhs_dim,), (rhs_dim,)), ((), ())), precision=HIGHEST, preferred_element_type=jnp.float32)


class RowSum:
    def __init__(self, members, sizes, part, out, pair_buf, acc, slots, sems):
        self.chips = members // 2
        me = lax.axis_index("rows")
        self.core, self.chip = lax.rem(me, 2), lax.div(me, 2)
        self.sizes = sizes
        self.starts = [sum(sizes[:g]) for g in range(len(sizes))]
        self.part, self.out, self.pair_buf, self.acc, self.slots = part, out, pair_buf, acc, slots
        self.swap_send, self.swap_recv, self.send, self.recv, self.back_send, self.back_recv, self.fwd_send, self.fwd_recv = sems

    def peer(self, d):
        return lax.rem(self.chip + d, self.chips)

    def pair_id(self):
        return {"rows": self.chip * 2 + 1 - self.core}

    def peer_id(self, d):
        return {"rows": self.peer(d) * 2 + self.core}

    def greet(self):
        barrier = pltpu.get_barrier_semaphore()
        pl.semaphore_signal(barrier, inc=1, device_id=self.pair_id(), device_id_type=MESH)
        for d in range(1, self.chips):
            pl.semaphore_signal(barrier, inc=1, device_id=self.peer_id(d), device_id_type=MESH)

    def await_all(self):
        pl.semaphore_wait(pltpu.get_barrier_semaphore(), self.chips)

    def half_rows(self, g, core):
        half = self.sizes[g] * BLK // 2
        return pl.ds(pl.multiple_of(self.starts[g] * BLK + core * half, 8), half)

    def chunk_of(self, g):
        return self.sizes[g] * BLK // (2 * self.chips)

    def own_rows(self, g, chip):
        half, chunk = self.sizes[g] * BLK // 2, self.chunk_of(g)
        return pl.ds(pl.multiple_of(self.starts[g] * BLK + self.core * half + chip * chunk, 8), chunk)

    def local_rows(self, g, chip):
        chunk = self.chunk_of(g)
        return pl.ds(pl.multiple_of(self.starts[g] * BLK // 2 + chip * chunk, 8), chunk)

    def local_half(self, g):
        return pl.ds(self.starts[g] * BLK // 2, self.sizes[g] * BLK // 2)

    def slot(self, g, d):
        chunk = self.chunk_of(g)
        base = self.starts[g] * BLK // (2 * self.chips)
        return self.slots.at[d - 1, pl.ds(base, chunk)]

    def swap(self, g):
        return pltpu.make_async_remote_copy(
            src_ref=self.part.at[self.half_rows(g, 1 - self.core)], dst_ref=self.pair_buf.at[self.local_half(g)],
            send_sem=self.swap_send.at[g], recv_sem=self.swap_recv.at[g], device_id=self.pair_id(), device_id_type=MESH)

    def scatter(self, g, d):
        return pltpu.make_async_remote_copy(
            src_ref=self.acc.at[self.local_rows(g, self.peer(d))], dst_ref=self.slot(g, d),
            send_sem=self.send.at[g, d - 1], recv_sem=self.recv.at[g, d - 1], device_id=self.peer_id(d), device_id_type=MESH)

    def gather(self, g, d):
        own = self.own_rows(g, self.chip)
        return pltpu.make_async_remote_copy(
            src_ref=self.out.at[own], dst_ref=self.out.at[own],
            send_sem=self.back_send.at[g, d - 1], recv_sem=self.back_recv.at[g, d - 1], device_id=self.peer_id(d), device_id_type=MESH)

    def forward(self, g, d):
        src = self.own_rows(g, self.peer(self.chips - d))
        return pltpu.make_async_remote_copy(
            src_ref=self.out.at[src], dst_ref=self.out.at[src],
            send_sem=self.fwd_send.at[g, d], recv_sem=self.fwd_recv.at[g, d], device_id=self.pair_id(), device_id_type=MESH)

    def start_swap(self, g):
        self.swap(g).start()

    def start_scatter(self, g):
        self.swap(g).wait()
        self.acc[self.local_half(g), :] = self.part[self.half_rows(g, self.core), :] + self.pair_buf[self.local_half(g), :]
        for d in range(1, self.chips):
            self.scatter(g, d).start()

    def start_gather(self, g):
        for d in range(1, self.chips):
            self.scatter(g, d).wait()
        total = self.acc[self.local_rows(g, self.chip), :]
        for d in range(1, self.chips):
            total = total + self.slot(g, d)[...]
        self.out[self.own_rows(g, self.chip), :] = total
        for d in range(1, self.chips):
            self.gather(g, d).start()
        self.forward(g, 0).start()

    def start_forward(self, g):
        for d in range(1, self.chips):
            self.gather(g, d).wait()
            self.forward(g, d).start()

    def drain(self, g):
        for d in range(self.chips):
            self.forward(g, d).wait()


def sum_scratch(members, sizes):
    chips = members // 2
    rows = sum(sizes) * BLK
    groups = len(sizes)
    sems = pltpu.SemaphoreType.DMA
    return [
        pltpu.VMEM((rows, BLK), jnp.float32), pltpu.VMEM((rows // 2, BLK), jnp.float32), pltpu.VMEM((rows // 2, BLK), jnp.float32),
        pltpu.VMEM((chips - 1, rows // (2 * chips), BLK), jnp.float32),
        sems((groups,)), sems((groups,)), sems((groups, chips - 1)), sems((groups, chips - 1)),
        sems((groups, chips - 1)), sems((groups, chips - 1)), sems((groups, chips)), sems((groups, chips)),
    ]


GRAM_GROUPS = (
    ((0, 2), (0, 3), (1, 2), (1, 3), (2, 2), (2, 3), (3, 3), (4, 2), (4, 3)),
    ((0, 0), (0, 1), (1, 1), (4, 0), (4, 1)),
    ((4, 4),),
)
BASIS_GROUPS = (
    ((0, 4), (1, 4), (2, 4), (3, 4), (4, 4)),
    ((0, 2), (0, 3), (1, 2), (1, 3), (2, 2), (2, 3), (3, 3)),
    ((0, 0), (0, 1), (1, 1)),
)


def proj_blocks(n):
    return -(-(n // 2) // BLK)


def block(idx):
    return slice(idx * BLK, (idx + 1) * BLK)


def pack_group(acc, part, start, pairs):
    for pos, (i, j) in enumerate(pairs):
        part[block(start + pos), :] = acc[block(i), block(j)] if i <= j else acc[block(i), block(j)].T


def tile_copy(src, dst, sem, t):
    rows = pl.ds(pl.multiple_of(t * ROW_TILE, ROW_TILE), ROW_TILE)
    return pltpu.make_async_copy(src.at[rows], dst.at[rows], sem.at[t])


def tile_rows(t):
    return pl.ds(pl.multiple_of(t * ROW_TILE, ROW_TILE), ROW_TILE)


def gram_kernel(members, a_hbm, out, a_buf, acc, load_sem, part, pair_buf, acc_half, slots, *sems):
    tiles = a_buf.shape[0] // ROW_TILE
    sizes = [len(group) for group in GRAM_GROUPS]
    total = RowSum(members, sizes, part, out, pair_buf, acc_half, slots, sems)
    total.greet()
    for t in range(tiles):
        tile_copy(a_hbm, a_buf, load_sem, t).start()
    acc[...] = jnp.zeros_like(acc)

    def first(t, carry):
        tile_copy(a_hbm, a_buf, load_sem, t).wait()
        rows = tile_rows(t)
        acc[:, 2 * BLK:4 * BLK] += dot_f32(a_buf[rows, :], a_buf[rows, 2 * BLK:4 * BLK], 0, 0)
        return carry

    lax.fori_loop(0, tiles, first, 0)
    pack_group(acc, part, total.starts[0], GRAM_GROUPS[0])
    total.await_all()
    total.start_swap(0)

    def second(t, carry):
        @pl.when(t == tiles // 4)
        def _():
            total.start_scatter(0)

        rows = tile_rows(t)
        rhs = a_buf[rows, :2 * BLK]
        acc[:2 * BLK, :2 * BLK] += dot_f32(rhs, rhs, 0, 0)
        acc[4 * BLK:, :2 * BLK] += dot_f32(a_buf[rows, 4 * BLK:], rhs, 0, 0)
        return carry

    lax.fori_loop(0, tiles, second, 0)
    pack_group(acc, part, total.starts[1], GRAM_GROUPS[1])
    total.start_swap(1)

    def third(t, carry):
        @pl.when(t == tiles // 4)
        def _():
            total.start_gather(0)

        @pl.when(t == tiles // 2)
        def _():
            total.start_scatter(1)

        last = a_buf[tile_rows(t), 4 * BLK:]
        acc[4 * BLK:, 4 * BLK:] += dot_f32(last, last, 0, 0)
        return carry

    lax.fori_loop(0, tiles, third, 0)
    pack_group(acc, part, total.starts[2], GRAM_GROUPS[2])
    total.start_swap(2)
    total.start_scatter(2)
    total.start_gather(1)
    total.start_forward(0)
    total.start_gather(2)
    total.start_forward(1)
    total.start_forward(2)
    for g in range(3):
        total.drain(g)


def gram_sum(a_blk, members, collective_id):
    m, n = a_blk.shape
    sizes = [len(group) for group in GRAM_GROUPS]
    return pl.pallas_call(
        functools.partial(gram_kernel, members),
        out_shape=jax.ShapeDtypeStruct((sum(sizes) * BLK, BLK), jnp.float32),
        in_specs=[pl.BlockSpec(memory_space=pl.ANY)],
        out_specs=pl.BlockSpec(memory_space=pltpu.VMEM),
        scratch_shapes=[pltpu.VMEM((m, n), jnp.float32), pltpu.VMEM((n, n), jnp.float32), pltpu.SemaphoreType.DMA((m // ROW_TILE,))] + sum_scratch(members, sizes),
        compiler_params=pltpu.CompilerParams(vmem_limit_bytes=VMEM_BYTES, collective_id=collective_id, has_side_effects=True),
        cost_estimate=pl.CostEstimate(flops=m * n * n * 6, bytes_accessed=4 * m * n, transcendentals=0),
        name="gram_one_sum",
    )(a_blk)


def basis_tile(a, inv, diag):
    left = dot_f32(a[:, :2 * BLK], inv[:2 * BLK, :2 * BLK], 1, 0)
    right = dot_f32(a[:, :4 * BLK], inv[:4 * BLK, 3 * BLK:], 1, 0)
    middle = dot_f32(a[:, :2 * BLK], inv[:2 * BLK, 2 * BLK:3 * BLK], 1, 0)
    ends = dot_f32(jnp.concatenate([a[:, 2 * BLK:3 * BLK], a[:, 4 * BLK:]], axis=1), diag[...], 1, 0)
    return left, middle + ends[:, :BLK], right[:, :BLK], right[:, BLK:] + ends[:, BLK:]


def basis_kernel(members, a_hbm, b_hbm, inv, out, a_buf, b_buf, diag, acc, acc_end, load_sem, b_sem, part, pair_buf, acc_half, slots, *sems):
    tiles = a_buf.shape[0] // ROW_TILE
    n, n_rhs = a_buf.shape[1], b_buf.shape[0]
    sizes = [len(group) for group in BASIS_GROUPS]
    n_end = sizes[0]
    sizes[0] += proj_blocks(n)
    total = RowSum(members, sizes, part, out, pair_buf, acc_half, slots, sems)
    total.greet()
    tile_copy(a_hbm, a_buf, load_sem, 0).start()
    b_copy = pltpu.make_async_copy(b_hbm, b_buf, b_sem)
    b_copy.start()
    for t in range(1, tiles):
        tile_copy(a_hbm, a_buf, load_sem, t).start()
    acc[...] = jnp.zeros_like(acc)
    acc_end[...] = jnp.zeros_like(acc_end)
    diag[...] = jnp.zeros_like(diag)
    diag[:BLK, :BLK] = inv[2 * BLK:3 * BLK, 2 * BLK:3 * BLK]
    diag[BLK:, BLK:] = inv[4 * BLK:, 4 * BLK:]
    b_copy.wait()

    def first(t, carry):
        tile_copy(a_hbm, a_buf, load_sem, t).wait()
        rows = tile_rows(t)
        left, third, fourth, fifth = basis_tile(a_buf[rows, :], inv, diag)
        a_buf[rows, :2 * BLK] = left
        a_buf[rows, 2 * BLK:3 * BLK] = third
        a_buf[rows, 3 * BLK:4 * BLK] = fourth
        a_buf[rows, 4 * BLK:] = fifth
        both = jnp.concatenate([fifth, b_buf[:, tile_rows(t)].T], axis=1)
        acc_end[...] += dot_f32(a_buf[rows, :], both, 0, 0)
        return carry

    lax.fori_loop(0, tiles, first, 0)
    for pos, (i, _) in enumerate(BASIS_GROUPS[0]):
        part[block(pos), :] = acc_end[block(i), :BLK]
    half = n // 2
    base = n_end * BLK
    part[base:base + half, :] = jnp.concatenate([acc_end[:half, BLK:], acc_end[half:, BLK:]], axis=1)
    if base + half < sizes[0] * BLK:
        part[base + half:sizes[0] * BLK, :] = jnp.zeros((sizes[0] * BLK - base - half, BLK), jnp.float32)
    total.await_all()
    total.start_swap(0)

    def second(t, carry):
        @pl.when(t == tiles // 4)
        def _():
            total.start_scatter(0)

        rows = tile_rows(t)
        acc[:, 2 * BLK:] += dot_f32(a_buf[rows, :4 * BLK], a_buf[rows, 2 * BLK:4 * BLK], 0, 0)
        return carry

    lax.fori_loop(0, tiles, second, 0)
    pack_group(acc, part, total.starts[1], BASIS_GROUPS[1])
    total.start_swap(1)
    total.start_gather(0)

    def third_part(t, carry):
        @pl.when(t == tiles // 4)
        def _():
            total.start_scatter(1)

        rows = tile_rows(t)
        rhs = a_buf[rows, :2 * BLK]
        acc[:2 * BLK, :2 * BLK] += dot_f32(rhs, rhs, 0, 0)
        return carry

    lax.fori_loop(0, tiles, third_part, 0)
    pack_group(acc, part, total.starts[2], BASIS_GROUPS[2])
    total.start_swap(2)
    total.start_scatter(2)
    total.start_forward(0)
    total.start_gather(1)
    total.start_gather(2)
    total.start_forward(1)
    total.start_forward(2)
    for g in range(3):
        total.drain(g)


def basis_sum(a_blk, b_blk, r_inv, members, collective_id):
    m, n = a_blk.shape
    n_rhs = b_blk.shape[1]
    sizes = [len(group) for group in BASIS_GROUPS]
    sizes[0] += proj_blocks(n)
    any_spec, vmem_spec = pl.BlockSpec(memory_space=pl.ANY), pl.BlockSpec(memory_space=pltpu.VMEM)
    return pl.pallas_call(
        functools.partial(basis_kernel, members),
        out_shape=jax.ShapeDtypeStruct((sum(sizes) * BLK, BLK), jnp.float32),
        in_specs=[any_spec, any_spec, vmem_spec],
        out_specs=vmem_spec,
        scratch_shapes=[
            pltpu.VMEM((m, n), jnp.float32), pltpu.VMEM((n_rhs, m), jnp.float32), pltpu.VMEM((2 * BLK, 2 * BLK), jnp.float32),
            pltpu.VMEM((4 * BLK, 4 * BLK), jnp.float32), pltpu.VMEM((n, BLK + n_rhs), jnp.float32),
            pltpu.SemaphoreType.DMA((m // ROW_TILE,)), pltpu.SemaphoreType.DMA,
        ] + sum_scratch(members, sizes),
        compiler_params=pltpu.CompilerParams(vmem_limit_bytes=VMEM_BYTES, collective_id=collective_id, has_side_effects=True),
        cost_estimate=pl.CostEstimate(flops=m * n * n * 12, bytes_accessed=4 * m * (n + n_rhs), transcendentals=0),
        name="basis_gram_two_sum",
    )(a_blk, b_blk.T, r_inv)


def row_of(arr, idx):
    return jnp.broadcast_to(arr[idx:idx + 1, :], (LEAF, arr.shape[1]))


def factor_block(sym):
    n_leaf = BLK // LEAF
    ahead = 2
    row_id = lax.broadcasted_iota(jnp.int32, (BLK, BLK), 0)
    col_id = lax.broadcasted_iota(jnp.int32, (BLK, BLK), 1)
    eye = (row_id == col_id).astype(jnp.float32)
    sub_id = lax.broadcasted_iota(jnp.int32, (LEAF, BLK), 0)
    s_rows = [sym[LEAF * t:LEAF * (t + 1), :] for t in range(n_leaf)]
    i_rows = [eye[LEAF * t:LEAF * (t + 1), :] for t in range(n_leaf)]
    for t in range(n_leaf):
        span = list(range(t, min(t + ahead + 1, n_leaf)))
        ecol = [[jnp.broadcast_to(s_rows[u][:, LEAF * t + i:LEAF * t + i + 1], (LEAF, BLK)) for u in span] for i in range(LEAF)]
        w_s, w_i = s_rows[t], i_rows[t]
        for i in range(LEAF):
            inv = lax.rsqrt(row_of(ecol[i][0], i))
            lcol = [e * inv for e in ecol[i]]
            bc_s = row_of(s_rows[t], i) * inv
            bc_i = row_of(i_rows[t], i) * inv
            w_s = jnp.where(sub_id == i, bc_s, w_s)
            w_i = jnp.where(sub_id == i, bc_i, w_i)
            for v, u in enumerate(span):
                if v == 0 and i == LEAF - 1:
                    continue
                s_rows[u] = s_rows[u] - lcol[v] * bc_s
                i_next = i_rows[u] - lcol[v] * bc_i
                i_rows[u] = i_next if v else jnp.where(sub_id > i, i_next, i_rows[u])
            for j in range(i + 1, LEAF):
                piv = row_of(lcol[0], j)
                ecol[j] = [e - c * piv for e, c in zip(ecol[j], lcol)]
        s_rows[t], i_rows[t] = w_s, w_i
        rest = t + ahead + 1
        if rest < n_leaf:
            upd = dot_f32(w_s, jnp.concatenate([w_s, w_i], axis=1), 0, 0)
            for u in range(rest, n_leaf):
                s_rows[u] = s_rows[u] - upd[LEAF * u:LEAF * (u + 1), :BLK]
                i_rows[u] = i_rows[u] - upd[LEAF * u:LEAF * (u + 1), BLK:]
    r_blk = jnp.where(row_id <= col_id, jnp.concatenate(s_rows, axis=0), 0.0)
    linv = jnp.where(row_id >= col_id, jnp.concatenate(i_rows, axis=0), 0.0)
    return r_blk, linv


def factor_all(work, r_out, n):
    n_blk = n // BLK

    def step(k, carry):
        base = pl.multiple_of(k * BLK, BLK)
        r_blk, linv = factor_block(work[pl.ds(base, BLK), pl.ds(base, BLK)])
        for kk in range(n_blk):
            @pl.when(k == kk)
            def _():
                lo, hi = BLK * kk, BLK * (kk + 1)
                if lo:
                    work[lo:hi, :lo] = dot_f32(linv, work[lo:hi, :lo], 1, 0)
                    r_out[lo:hi, :lo] = jnp.zeros((BLK, lo), jnp.float32)
                work[lo:hi, lo:hi] = linv
                r_out[lo:hi, lo:hi] = r_blk
                if hi < n:
                    r_row = dot_f32(linv, work[lo:hi, hi:], 1, 0)
                    r_out[lo:hi, hi:] = r_row
                    work[lo:hi, hi:] = jnp.zeros((BLK, n - hi), jnp.float32)
                    for ii in range(kk + 1, n_blk):
                        a, b = BLK * ii, BLK * (ii + 1)
                        fac = r_row[:, a - hi:b - hi]
                        work[a:b, a:] = work[a:b, a:] - dot_f32(fac, r_row[:, a - hi:], 0, 0)
                        if lo:
                            work[a:b, :lo] = work[a:b, :lo] - dot_f32(fac, work[lo:hi, :lo], 0, 0)
                        work[a:b, lo:hi] = -dot_f32(fac, linv, 0, 0)
        return carry

    lax.fori_loop(0, n_blk, step, 0)


def unpack_upper(packed, work, groups, skip):
    start = 0
    for group in groups:
        for pos, (i, j) in enumerate(group):
            lo, hi = min(i, j), max(i, j)
            work[block(lo), block(hi)] = packed[block(start + pos), :]
        start += len(group) + (skip if group is groups[0] else 0)


def factor_kernel(packed, r_out, inv_out, work):
    n = work.shape[0]
    unpack_upper(packed, work, GRAM_GROUPS, 0)
    factor_all(work, r_out, n)
    for c in range(0, n, BLK):
        inv_out[:, c:c + BLK] = work[c:c + BLK, :].T


def factor_one(packed, n):
    return pl.pallas_call(
        factor_kernel,
        out_shape=[jax.ShapeDtypeStruct((n, n), jnp.float32)] * 2,
        in_specs=[pl.BlockSpec(memory_space=pltpu.VMEM)],
        out_specs=[pl.BlockSpec(memory_space=pltpu.VMEM)] * 2,
        scratch_shapes=[pltpu.VMEM((n, n), jnp.float32)],
        name="factor_one",
    )(packed)


def finish_kernel(packed, r_one, inv_one, x_out, r_out, work, r_two):
    n_rhs, n = x_out.shape
    unpack_upper(packed, work, BASIS_GROUPS, proj_blocks(n))
    factor_all(work, r_two, n)
    base = len(BASIS_GROUPS[0]) * BLK
    half = n // 2
    flat = packed[base:base + half, :]
    proj = jnp.concatenate([flat[:, :n_rhs], flat[:, n_rhs:]], axis=0)
    proj_two = dot_f32(work[...], proj, 1, 0)
    back = dot_f32(work[...], proj_two, 0, 0)
    x_out[...] = dot_f32(inv_one[...], back, 1, 0).T
    for lo in range(0, n, BLK):
        hi = lo + BLK
        if lo:
            r_out[lo:hi, :lo] = jnp.zeros((BLK, lo), jnp.float32)
        r_out[lo:hi, lo:] = dot_f32(r_two[lo:hi, lo:], r_one[lo:, lo:], 1, 0)


def finish(packed, r_one, inv_one, n_rhs):
    n = r_one.shape[0]
    return pl.pallas_call(
        finish_kernel,
        out_shape=[jax.ShapeDtypeStruct((n_rhs, n), jnp.float32), jax.ShapeDtypeStruct((n, n), jnp.float32)],
        in_specs=[pl.BlockSpec(memory_space=pltpu.VMEM)] * 3,
        out_specs=[pl.BlockSpec(memory_space=pltpu.VMEM)] * 2,
        scratch_shapes=[pltpu.VMEM((n, n), jnp.float32)] * 2,
        name="finish",
    )(packed, r_one, inv_one)


def solution(mesh):
    members = mesh.shape["rows"]

    def group_solve(a_blk, b_blk):
        n, n_rhs = a_blk.shape[1], b_blk.shape[1]
        gram_one = gram_sum(a_blk, members, 1)
        r_one, inv_one = factor_one(gram_one, n)
        gram_two = basis_sum(a_blk, b_blk, inv_one, members, 2)
        x_flat, r_factor = finish(gram_two, r_one, inv_one, n_rhs)
        return x_flat.T, r_factor

    row_spec = P(("batch", "rows"), None)
    out_spec = P("batch", None)
    return jax.shard_map(group_solve, mesh=mesh, in_specs=(row_spec, row_spec), out_specs=(out_spec, out_spec), check_vma=False)
```

time: 975 us -> 256 us (0.26); the launches traced: 964 us -> 256 us
  other arithmetic: 364 us -> 0 us
  matrix products: 302 us -> 0 us
  Pallas kernels: 0 us -> 255 us
  waiting for transfers between devices: 221 us -> 0 us
  local copies, waits for them, and re-layouts: 56.2 us -> 0 us
  between operations: 21.3 us -> 0.65 us
    another operation x43 -> x0, other arithmetic: 360 us -> none  [the longest x19 104 us: group_solve(): low_two = jnp.linalg.cholesky(gram_two)]
    pallas_call x0 -> x4, Pallas kernels: none -> 255 us  [the longest x1 115 us: basis_sum(): pl.pallas_call(functools.partial(basis_kernel, members), out_shape=jax.Sh...]
    psum x2 -> x0, waiting for transfers between devices: 221 us -> none  [the longest x1 112 us: group_solve(): gram_one = lax.psum(gram_of(a_blk, a_blk), 'rows')]
    another operation x43 -> x0, matrix products: 155 us -> none  [the longest x9 122 us: group_solve(): lax.linalg.triangular_solve(low_one, a_blk, left_side=False, lower=True,...]
    dot_general x4 -> x0, matrix products: 147 us -> none  [the longest x3 138 us: gram_of(): lax.dot_general(left_mat, right_mat, (((0,), (0,)), ((), ())), precision=...]
    another operation x57 -> x0, local copies, waits for them, and re-layouts: 45.1 us -> none
  transfers between devices with their start and end apart: 2 -> 0, of which waited for: 2 -> 0; matrix products, arithmetic and copies ran while one was open for 0% -> 0% of each run, Pallas kernels for 0% -> 0%
where the time goes in v2:
time: 256 us
  Pallas kernels  255 us (100%)
    pallas_call x1, Pallas kernels, basis_sum(): pl.pallas_call(functools.partial(basis_kernel, members), out_shape=jax.Sh...  115 us
    pallas_call x1, Pallas kernels, gram_sum(): pl.pallas_call(functools.partial(gram_kernel, members), out_shape=jax.Sha...  70 us
    pallas_call x1, Pallas kernels, finish(): pl.pallas_call(finish_kernel, out_shape=[jax.ShapeDtypeStruct((n_rhs, n),...  39.3 us
    pallas_call x1, Pallas kernels, factor_one(): pl.pallas_call(factor_kernel, out_shape=[jax.ShapeDtypeStruct((n, n), jnp...  30.7 us

profile of v2, /device:TPU:21, one launch (start us, length us, event | category | flops | bytes accessed | tf_op | source)
XLA Modules:
  0.0 255.8 jit_solution(12155744807567788028)
XLA Ops:
  0.6 70.0 %gram_one_sum.1.packed = f32[1920,128]{1,0:T(8,128)} custom-call(f32[8192,640]{1,0:T(8,128)} %a_hbm.3), custom_call_target="tpu_custom_call" | custom-call | flops 20132659200 | bytes 20971520 | tf_op jit(solution)/shard_map/gram_one_sum/pallas_call | solution.py:235
  70.6 30.7 %factor_one.1 = (f32[640,640]{1,0:T(8,128)}, f32[640,640]{1,0:T(8,128)}) custom-call(f32[1920,128]{1,0:T(8,128)} %gram_one_sum.1.packed), custom_call_target="tpu_custom_call" | custom-call | tf_op jit(solution)/shard_map/factor_one/pallas_call | solution.py:451
  101.3 115.2 %basis_gram_two_sum.1.packed = f32[2304,128]{1,0:T(8,128)} custom-call(f32[8192,640]{1,0:T(8,128)} %a_hbm.3, f32[64,8192]{1,0:T(8,128)} %bitcast.2, f32[640,640]{1,0:T(8,128)} %get-tuple-element.6.inv.inv_one), custom_call_target="tpu_custom_call" | custom-call | flops 40265318400 | bytes 23068672 | tf_op jit(solution)/shard_map/basis_gram_two_sum/pallas_call | solution.py:341
  216.5 39.3 %finish.1 = (f32[64,640]{1,0:T(8,128)}, f32[640,640]{1,0:T(8,128)}) custom-call(f32[2304,128]{1,0:T(8,128)} %basis_gram_two_sum.1.packed, f32[640,640]{1,0:T(8,128)} %get-tuple-element.7.r_one, f32[640,640]{1,0:T(8,128)} %get-tuple-element.6.inv.inv_one), custom_call_target="tpu_custom_call" | custom-call | tf_op jit(solution)/shard_map/finish/pallas_call | solution.py:481

commit v3 on v2

--- a/solution.py
+++ b/solution.py
@@ -9,8 +9,11 @@
 HIGHEST = lax.Precision.HIGHEST
 MESH = pl.DeviceIdType.MESH
 LEAF = 8
+GROUP = 2
+AHEAD = 2
 BLK = 128
-ROW_TILE = 512
+GRAM_TILES = (512, 1024, 1024)
+BASIS_TILES = (512, 1024, 1024)
 VMEM_BYTES = 64000 * 1024
 
 
@@ -159,27 +162,28 @@
         part[block(start + pos), :] = acc[block(i), block(j)] if i <= j else acc[block(i), block(j)].T
 
 
-def tile_copy(src, dst, sem, t):
-    rows = pl.ds(pl.multiple_of(t * ROW_TILE, ROW_TILE), ROW_TILE)
+def tile_rows(t, size):
+    return pl.ds(pl.multiple_of(t * size, size), size)
+
+
+def tile_copy(src, dst, sem, t, size):
+    rows = tile_rows(t, size)
     return pltpu.make_async_copy(src.at[rows], dst.at[rows], sem.at[t])
 
 
-def tile_rows(t):
-    return pl.ds(pl.multiple_of(t * ROW_TILE, ROW_TILE), ROW_TILE)
-
-
 def gram_kernel(members, a_hbm, out, a_buf, acc, load_sem, part, pair_buf, acc_half, slots, *sems):
-    tiles = a_buf.shape[0] // ROW_TILE
+    first_size, second_size, third_size = GRAM_TILES
+    tiles = a_buf.shape[0] // first_size
     sizes = [len(group) for group in GRAM_GROUPS]
     total = RowSum(members, sizes, part, out, pair_buf, acc_half, slots, sems)
     total.greet()
     for t in range(tiles):
-        tile_copy(a_hbm, a_buf, load_sem, t).start()
+        tile_copy(a_hbm, a_buf, load_sem, t, first_size).start()
     acc[...] = jnp.zeros_like(acc)
 
     def first(t, carry):
-        tile_copy(a_hbm, a_buf, load_sem, t).wait()
-        rows = tile_rows(t)
+        tile_copy(a_hbm, a_buf, load_sem, t, first_size).wait()
+        rows = tile_rows(t, first_size)
         acc[:, 2 * BLK:4 * BLK] += dot_f32(a_buf[rows, :], a_buf[rows, 2 * BLK:4 * BLK], 0, 0)
         return carry
 
@@ -189,34 +193,34 @@
     total.start_swap(0)
 
     def second(t, carry):
-        @pl.when(t == tiles // 4)
+        @pl.when(t == 1)
         def _():
             total.start_scatter(0)
 
-        rows = tile_rows(t)
+        rows = tile_rows(t, second_size)
         rhs = a_buf[rows, :2 * BLK]
         acc[:2 * BLK, :2 * BLK] += dot_f32(rhs, rhs, 0, 0)
         acc[4 * BLK:, :2 * BLK] += dot_f32(a_buf[rows, 4 * BLK:], rhs, 0, 0)
         return carry
 
-    lax.fori_loop(0, tiles, second, 0)
+    lax.fori_loop(0, a_buf.shape[0] // second_size, second, 0)
     pack_group(acc, part, total.starts[1], GRAM_GROUPS[1])
     total.start_swap(1)
 
     def third(t, carry):
-        @pl.when(t == tiles // 4)
+        @pl.when(t == 0)
         def _():
             total.start_gather(0)
 
-        @pl.when(t == tiles // 2)
+        @pl.when(t == 3)
         def _():
             total.start_scatter(1)
 
-        last = a_buf[tile_rows(t), 4 * BLK:]
+        last = a_buf[tile_rows(t, third_size), 4 * BLK:]
         acc[4 * BLK:, 4 * BLK:] += dot_f32(last, last, 0, 0)
         return carry
 
-    lax.fori_loop(0, tiles, third, 0)
+    lax.fori_loop(0, a_buf.shape[0] // third_size, third, 0)
     pack_group(acc, part, total.starts[2], GRAM_GROUPS[2])
     total.start_swap(2)
     total.start_scatter(2)
@@ -237,7 +241,7 @@
         out_shape=jax.ShapeDtypeStruct((sum(sizes) * BLK, BLK), jnp.float32),
         in_specs=[pl.BlockSpec(memory_space=pl.ANY)],
         out_specs=pl.BlockSpec(memory_space=pltpu.VMEM),
-        scratch_shapes=[pltpu.VMEM((m, n), jnp.float32), pltpu.VMEM((n, n), jnp.float32), pltpu.SemaphoreType.DMA((m // ROW_TILE,))] + sum_scratch(members, sizes),
+        scratch_shapes=[pltpu.VMEM((m, n), jnp.float32), pltpu.VMEM((n, n), jnp.float32), pltpu.SemaphoreType.DMA((m // GRAM_TILES[0],))] + sum_scratch(members, sizes),
         compiler_params=pltpu.CompilerParams(vmem_limit_bytes=VMEM_BYTES, collective_id=collective_id, has_side_effects=True),
         cost_estimate=pl.CostEstimate(flops=m * n * n * 6, bytes_accessed=4 * m * n, transcendentals=0),
         name="gram_one_sum",
@@ -253,18 +257,19 @@
 
 
 def basis_kernel(members, a_hbm, b_hbm, inv, out, a_buf, b_buf, diag, acc, acc_end, load_sem, b_sem, part, pair_buf, acc_half, slots, *sems):
-    tiles = a_buf.shape[0] // ROW_TILE
+    first_size, second_size, third_size = BASIS_TILES
+    tiles = a_buf.shape[0] // first_size
     n, n_rhs = a_buf.shape[1], b_buf.shape[0]
     sizes = [len(group) for group in BASIS_GROUPS]
     n_end = sizes[0]
     sizes[0] += proj_blocks(n)
     total = RowSum(members, sizes, part, out, pair_buf, acc_half, slots, sems)
     total.greet()
-    tile_copy(a_hbm, a_buf, load_sem, 0).start()
+    tile_copy(a_hbm, a_buf, load_sem, 0, first_size).start()
     b_copy = pltpu.make_async_copy(b_hbm, b_buf, b_sem)
     b_copy.start()
     for t in range(1, tiles):
-        tile_copy(a_hbm, a_buf, load_sem, t).start()
+        tile_copy(a_hbm, a_buf, load_sem, t, first_size).start()
     acc[...] = jnp.zeros_like(acc)
     acc_end[...] = jnp.zeros_like(acc_end)
     diag[...] = jnp.zeros_like(diag)
@@ -273,14 +278,14 @@
     b_copy.wait()
 
     def first(t, carry):
-        tile_copy(a_hbm, a_buf, load_sem, t).wait()
-        rows = tile_rows(t)
+        tile_copy(a_hbm, a_buf, load_sem, t, first_size).wait()
+        rows = tile_rows(t, first_size)
         left, third, fourth, fifth = basis_tile(a_buf[rows, :], inv, diag)
         a_buf[rows, :2 * BLK] = left
         a_buf[rows, 2 * BLK:3 * BLK] = third
         a_buf[rows, 3 * BLK:4 * BLK] = fourth
         a_buf[rows, 4 * BLK:] = fifth
-        both = jnp.concatenate([fifth, b_buf[:, tile_rows(t)].T], axis=1)
+        both = jnp.concatenate([fifth, b_buf[:, tile_rows(t, first_size)].T], axis=1)
         acc_end[...] += dot_f32(a_buf[rows, :], both, 0, 0)
         return carry
 
@@ -296,30 +301,33 @@
     total.start_swap(0)
 
     def second(t, carry):
-        @pl.when(t == tiles // 4)
+        @pl.when(t == 1)
         def _():
             total.start_scatter(0)
 
-        rows = tile_rows(t)
+        @pl.when(t == 6)
+        def _():
+            total.start_gather(0)
+
+        rows = tile_rows(t, second_size)
         acc[:, 2 * BLK:] += dot_f32(a_buf[rows, :4 * BLK], a_buf[rows, 2 * BLK:4 * BLK], 0, 0)
         return carry
 
-    lax.fori_loop(0, tiles, second, 0)
+    lax.fori_loop(0, a_buf.shape[0] // second_size, second, 0)
     pack_group(acc, part, total.starts[1], BASIS_GROUPS[1])
     total.start_swap(1)
-    total.start_gather(0)
 
     def third_part(t, carry):
-        @pl.when(t == tiles // 4)
+        @pl.when(t == 1)
         def _():
             total.start_scatter(1)
 
-        rows = tile_rows(t)
+        rows = tile_rows(t, third_size)
         rhs = a_buf[rows, :2 * BLK]
         acc[:2 * BLK, :2 * BLK] += dot_f32(rhs, rhs, 0, 0)
         return carry
 
-    lax.fori_loop(0, tiles, third_part, 0)
+    lax.fori_loop(0, a_buf.shape[0] // third_size, third_part, 0)
     pack_group(acc, part, total.starts[2], BASIS_GROUPS[2])
     total.start_swap(2)
     total.start_scatter(2)
@@ -346,7 +354,7 @@
         scratch_shapes=[
             pltpu.VMEM((m, n), jnp.float32), pltpu.VMEM((n_rhs, m), jnp.float32), pltpu.VMEM((2 * BLK, 2 * BLK), jnp.float32),
             pltpu.VMEM((4 * BLK, 4 * BLK), jnp.float32), pltpu.VMEM((n, BLK + n_rhs), jnp.float32),
-            pltpu.SemaphoreType.DMA((m // ROW_TILE,)), pltpu.SemaphoreType.DMA,
+            pltpu.SemaphoreType.DMA((m // BASIS_TILES[0],)), pltpu.SemaphoreType.DMA,
         ] + sum_scratch(members, sizes),
         compiler_params=pltpu.CompilerParams(vmem_limit_bytes=VMEM_BYTES, collective_id=collective_id, has_side_effects=True),
         cost_estimate=pl.CostEstimate(flops=m * n * n * 12, bytes_accessed=4 * m * (n + n_rhs), transcendentals=0),
@@ -360,37 +368,40 @@
 
 def factor_block(sym):
     n_leaf = BLK // LEAF
-    ahead = 2
     row_id = lax.broadcasted_iota(jnp.int32, (BLK, BLK), 0)
     col_id = lax.broadcasted_iota(jnp.int32, (BLK, BLK), 1)
     eye = (row_id == col_id).astype(jnp.float32)
     sub_id = lax.broadcasted_iota(jnp.int32, (LEAF, BLK), 0)
     s_rows = [sym[LEAF * t:LEAF * (t + 1), :] for t in range(n_leaf)]
     i_rows = [eye[LEAF * t:LEAF * (t + 1), :] for t in range(n_leaf)]
-    for t in range(n_leaf):
-        span = list(range(t, min(t + ahead + 1, n_leaf)))
-        ecol = [[jnp.broadcast_to(s_rows[u][:, LEAF * t + i:LEAF * t + i + 1], (LEAF, BLK)) for u in span] for i in range(LEAF)]
-        w_s, w_i = s_rows[t], i_rows[t]
-        for i in range(LEAF):
-            inv = lax.rsqrt(row_of(ecol[i][0], i))
-            lcol = [e * inv for e in ecol[i]]
-            bc_s = row_of(s_rows[t], i) * inv
-            bc_i = row_of(i_rows[t], i) * inv
-            w_s = jnp.where(sub_id == i, bc_s, w_s)
-            w_i = jnp.where(sub_id == i, bc_i, w_i)
-            for v, u in enumerate(span):
-                if v == 0 and i == LEAF - 1:
+    for t in range(0, n_leaf, GROUP):
+        first = LEAF * t
+        span = list(range(t, min(t + GROUP + AHEAD, n_leaf)))
+        ecol = [[jnp.broadcast_to(s_rows[u][:, first + j:first + j + 1], (LEAF, BLK)) if u >= t + j // LEAF else None for u in span] for j in range(GROUP * LEAF)]
+        done_s, done_i = list(s_rows[t:t + GROUP]), list(i_rows[t:t + GROUP])
+        for i in range(GROUP * LEAF):
+            v0, sub = i // LEAF, i % LEAF
+            inv = lax.rsqrt(row_of(ecol[i][v0], sub))
+            lcol = [None] * v0 + [e * inv for e in ecol[i][v0:]]
+            bc_s = row_of(s_rows[t + v0], sub) * inv
+            bc_i = row_of(i_rows[t + v0], sub) * inv
+            done_s[v0] = jnp.where(sub_id == sub, bc_s, done_s[v0])
+            done_i[v0] = jnp.where(sub_id == sub, bc_i, done_i[v0])
+            for v in range(v0, len(span)):
+                if v == v0 and sub == LEAF - 1:
                     continue
+                u = span[v]
                 s_rows[u] = s_rows[u] - lcol[v] * bc_s
-                i_next = i_rows[u] - lcol[v] * bc_i
-                i_rows[u] = i_next if v else jnp.where(sub_id > i, i_next, i_rows[u])
-            for j in range(i + 1, LEAF):
-                piv = row_of(lcol[0], j)
-                ecol[j] = [e - c * piv for e, c in zip(ecol[j], lcol)]
-        s_rows[t], i_rows[t] = w_s, w_i
-        rest = t + ahead + 1
+                i_rows[u] = i_rows[u] - lcol[v] * bc_i
+            for j in range(i + 1, GROUP * LEAF):
+                piv = row_of(lcol[j // LEAF], j % LEAF)
+                for v in range(j // LEAF, len(span)):
+                    ecol[j][v] = ecol[j][v] - lcol[v] * piv
+        s_rows[t:t + GROUP], i_rows[t:t + GROUP] = done_s, done_i
+        rest = t + GROUP + AHEAD
         if rest < n_leaf:
-            upd = dot_f32(w_s, jnp.concatenate([w_s, w_i], axis=1), 0, 0)
+            w_s = jnp.concatenate(done_s, axis=0)
+            upd = dot_f32(w_s, jnp.concatenate([w_s, jnp.concatenate(done_i, axis=0)], axis=1), 0, 0)
             for u in range(rest, n_leaf):
                 s_rows[u] = s_rows[u] - upd[LEAF * u:LEAF * (u + 1), :BLK]
                 i_rows[u] = i_rows[u] - upd[LEAF * u:LEAF * (u + 1), BLK:]

time: 256 us -> 236 us (0.922)
  Pallas kernels: 255 us -> 234 us
    pallas_call x1, Pallas kernels: 39.3 us -> 32.7 us  [finish(): pl.pallas_call(finish_kernel, out_shape=[jax.ShapeDtypeStruct((n_rhs, n),...]
    pallas_call x1, Pallas kernels: 30.7 us -> 24.2 us  [factor_one(): pl.pallas_call(factor_kernel, out_shape=[jax.ShapeDtypeStruct((n, n), jnp...]
    pallas_call x1, Pallas kernels: 115 us -> 110 us  [basis_sum(): pl.pallas_call(functools.partial(basis_kernel, members), out_shape=jax.Sh...]
    pallas_call x1, Pallas kernels: 70 us -> 67 us  [gram_sum(): pl.pallas_call(functools.partial(gram_kernel, members), out_shape=jax.Sha...]
where the time goes in v3:
time: 236 us; the launch traced here: 235 us
  Pallas kernels  234 us (99%)
    pallas_call x1, Pallas kernels, basis_sum(): pl.pallas_call(functools.partial(basis_kernel, members), out_shape=jax.Sh...  110 us
    pallas_call x1, Pallas kernels, gram_sum(): pl.pallas_call(functools.partial(gram_kernel, members), out_shape=jax.Sha...  67 us
    pallas_call x1, Pallas kernels, finish(): pl.pallas_call(finish_kernel, out_shape=[jax.ShapeDtypeStruct((n_rhs, n),...  32.7 us
    pallas_call x1, Pallas kernels, factor_one(): pl.pallas_call(factor_kernel, out_shape=[jax.ShapeDtypeStruct((n, n), jnp...  24.2 us

profile of v3, /device:TPU:21, one launch (start us, length us, event | category | flops | bytes accessed | tf_op | source)
XLA Modules:
  0.0 235.1 jit_solution(15225656077651908575)
XLA Ops:
  0.6 67.0 %gram_one_sum.1.packed = f32[1920,128]{1,0:T(8,128)} custom-call(f32[8192,640]{1,0:T(8,128)} %a_hbm.3), custom_call_target="tpu_custom_call" | custom-call | flops 20132659200 | bytes 20971520 | tf_op jit(solution)/shard_map/gram_one_sum/pallas_call | solution.py:239
  67.7 24.2 %factor_one.1 = (f32[640,640]{1,0:T(8,128)}, f32[640,640]{1,0:T(8,128)}) custom-call(f32[1920,128]{1,0:T(8,128)} %gram_one_sum.1.packed), custom_call_target="tpu_custom_call" | custom-call | tf_op jit(solution)/shard_map/factor_one/pallas_call | solution.py:462
  91.9 110.5 %basis_gram_two_sum.1.packed = f32[2304,128]{1,0:T(8,128)} custom-call(f32[8192,640]{1,0:T(8,128)} %a_hbm.3, f32[64,8192]{1,0:T(8,128)} %bitcast.2, f32[640,640]{1,0:T(8,128)} %get-tuple-element.6.inv.inv_one), custom_call_target="tpu_custom_call" | custom-call | flops 40265318400 | bytes 23068672 | tf_op jit(solution)/shard_map/basis_gram_two_sum/pallas_call | solution.py:349
  202.3 32.7 %finish.1 = (f32[64,640]{1,0:T(8,128)}, f32[640,640]{1,0:T(8,128)}) custom-call(f32[2304,128]{1,0:T(8,128)} %basis_gram_two_sum.1.packed, f32[640,640]{1,0:T(8,128)} %get-tuple-element.7.r_one, f32[640,640]{1,0:T(8,128)} %get-tuple-element.6.inv.inv_one), custom_call_target="tpu_custom_call" | custom-call | tf_op jit(solution)/shard_map/finish/pallas_call | solution.py:492

commit v4 on v3

--- a/solution.py
+++ b/solution.py
@@ -12,8 +12,8 @@
 GROUP = 2
 AHEAD = 2
 BLK = 128
-GRAM_TILES = (512, 1024, 1024)
-BASIS_TILES = (512, 1024, 1024)
+GRAM_TILES = (1024, 1024, 1024)
+BASIS_TILES = (512, 1024, 2048)
 VMEM_BYTES = 64000 * 1024
 
 
@@ -476,10 +476,10 @@
     base = len(BASIS_GROUPS[0]) * BLK
     half = n // 2
     flat = packed[base:base + half, :]
-    proj = jnp.concatenate([flat[:, :n_rhs], flat[:, n_rhs:]], axis=0)
-    proj_two = dot_f32(work[...], proj, 1, 0)
-    back = dot_f32(work[...], proj_two, 0, 0)
-    x_out[...] = dot_f32(inv_one[...], back, 1, 0).T
+    proj = jnp.concatenate([flat[:, :n_rhs].T, flat[:, n_rhs:].T], axis=1)
+    proj_two = dot_f32(proj, work[...], 1, 1)
+    back = dot_f32(proj_two, work[...], 1, 0)
+    x_out[...] = dot_f32(back, inv_one[...], 1, 1)
     for lo in range(0, n, BLK):
         hi = lo + BLK
         if lo:

time: 236 us -> 229 us (0.970)
  Pallas kernels: 234 us -> 228 us
    pallas_call x1, Pallas kernels: 67 us -> 64.3 us  [gram_sum(): pl.pallas_call(functools.partial(gram_kernel, members), out_shape=jax.Sha...]
where the time goes in v4:
time: 229 us
  Pallas kernels  228 us (100%)
    pallas_call x1, Pallas kernels, basis_sum(): pl.pallas_call(functools.partial(basis_kernel, members), out_shape=jax.Sh...  109 us
    pallas_call x1, Pallas kernels, gram_sum(): pl.pallas_call(functools.partial(gram_kernel, members), out_shape=jax.Sha...  64.3 us
    pallas_call x1, Pallas kernels, finish(): pl.pallas_call(finish_kernel, out_shape=[jax.ShapeDtypeStruct((n_rhs, n),...  30.5 us
    pallas_call x1, Pallas kernels, factor_one(): pl.pallas_call(factor_kernel, out_shape=[jax.ShapeDtypeStruct((n, n), jnp...  24.2 us

profile of v4, /device:TPU:21, one launch (start us, length us, event | category | flops | bytes accessed | tf_op | source)
XLA Modules:
  0.0 228.6 jit_solution(10098616936494119866)
XLA Ops:
  0.6 64.3 %gram_one_sum.1.packed = f32[1920,128]{1,0:T(8,128)} custom-call(f32[8192,640]{1,0:T(8,128)} %a_hbm.3), custom_call_target="tpu_custom_call" | custom-call | flops 20132659200 | bytes 20971520 | tf_op jit(solution)/shard_map/gram_one_sum/pallas_call | solution.py:239
  65.0 24.2 %factor_one.1 = (f32[640,640]{1,0:T(8,128)}, f32[640,640]{1,0:T(8,128)}) custom-call(f32[1920,128]{1,0:T(8,128)} %gram_one_sum.1.packed), custom_call_target="tpu_custom_call" | custom-call | tf_op jit(solution)/shard_map/factor_one/pallas_call | solution.py:462
  89.1 108.9 %basis_gram_two_sum.1.packed = f32[2304,128]{1,0:T(8,128)} custom-call(f32[8192,640]{1,0:T(8,128)} %a_hbm.3, f32[64,8192]{1,0:T(8,128)} %bitcast.2, f32[640,640]{1,0:T(8,128)} %get-tuple-element.6.inv.inv_one), custom_call_target="tpu_custom_call" | custom-call | flops 40265318400 | bytes 23068672 | tf_op jit(solution)/shard_map/basis_gram_two_sum/pallas_call | solution.py:349
  198.1 30.5 %finish.1 = (f32[64,640]{1,0:T(8,128)}, f32[640,640]{1,0:T(8,128)}) custom-call(f32[2304,128]{1,0:T(8,128)} %basis_gram_two_sum.1.packed, f32[640,640]{1,0:T(8,128)} %get-tuple-element.7.r_one, f32[640,640]{1,0:T(8,128)} %get-tuple-element.6.inv.inv_one), custom_call_target="tpu_custom_call" | custom-call | tf_op jit(solution)/shard_map/finish/pallas_call | solution.py:492
